TPU v7x, 256 devices: a whole 4x4x8 slice. The times are simulated.
256 devices in a mesh: dp: 32 (over z_lo, x, y), mp: 8 (over z_hi, core).
Axes of the slice: x: 4, y: 4, z: 8 (z_hi: 4, z_lo: 2; z = z_hi * 2 + z_lo), core: 2. Of those that a mesh axis runs over, the one named last changes fastest.
Arguments:
- hidden_states: bfloat16 [16384, 4096], P('dp', 'mp'), may hold values from -40 to 40
- norm_gain: float32 [1, 4096], replicated, may hold values from 0.1 to 1.9
- query_weight: bfloat16 [1, 4096, 4096], P(None, 'dp', 'mp'), may hold values from -0.01171875 to 0.01171875
- keyvalue_weight: bfloat16 [1, 4096, 2, 4096], P(None, 'dp', None, 'mp'), may hold values from -0.09375 to 0.09375
- output_weight: bfloat16 [1, 4096, 4096], P(None, 'dp', 'mp'), may hold values from -0.09375 to 0.09375
- position_bias: float32 [1, 32, 64], P(None, None, 'mp'), may hold values from -8 to 250
- lengths: int32 [128], P('dp'), may hold values from 16 to 128
Outputs:
- layer_output: bfloat16 [16384, 4096], P('dp', 'mp')
All inputs are finite; a program needn't handle non-finite values.
Results may differ from a plain program's by a relative error of at most 0.006.
Values may be sent and summed in bfloat16 or wider, within the bound.
A program may use at most 128 MiB of HBM per device.

v0:
```python
import jax
import jax.numpy as jnp
import numpy as np
from jax import lax
from jax.sharding import PartitionSpec as P

DH = 64
BUCKETS = 32
DIST = 128
LEN = 128
epsilon = 1e-06


def side_by_side(arrays, axis, dim, along):
    columns = [a.reshape(*a.shape[:along], -1) for a in arrays]
    both = jnp.concatenate(columns, axis=along)
    filled, at, outs = (lax.all_gather(both, axis, axis=dim, tiled=True), 0, [])
    for a, column in zip(arrays, columns):
        piece = filled[..., at : at + column.shape[along]]
        outs.append(piece.reshape(*piece.shape[:along], *a.shape[along:]))
        at += column.shape[along]
    return tuple(outs)


def bucket_table():
    half_count = BUCKETS // 2
    exact_count = half_count // 2
    positions = np.arange(LEN)
    relative = positions[None, :] - positions[:, None]
    distance = np.abs(relative)
    scaled = (
        np.log(np.maximum(distance, 1) / exact_count)
        / np.log(DIST / exact_count)
        * (half_count - exact_count)
    )
    far_bucket = np.minimum(exact_count + np.floor(scaled + 1e-09).astype(np.int32), half_count - 1)
    near_bucket = np.where(distance < exact_count, distance, far_bucket)
    return (near_bucket + np.where(relative > 0, half_count, 0)).astype(np.int32)


def normed_rows(hidden, gain_row):
    values = hidden.astype(jnp.float32)
    mean_square = jnp.mean(values * values, axis=-1, keepdims=True)
    return (values * lax.rsqrt(mean_square + epsilon) * gain_row).astype(jnp.bfloat16)


def add_projections(query_acc, pair_acc, normed, query_piece, pair_piece):
    query_acc = jnp.dot(normed, query_piece, preferred_element_type=jnp.float32)
    pair_acc = jnp.einsum("td,dcf->ctf", normed, pair_piece, preferred_element_type=jnp.float32)
    return (query_acc, pair_acc)


def local(
    hidden_states, norm_gain, query_weight, keyvalue_weight, output_weight, position_bias, lengths
):
    captions = lengths.shape[0]
    tokens_here = hidden_states.shape[0]
    heads_here = position_bias.shape[2]
    inner_here = heads_here * DH
    bucket_onehot = jnp.asarray(
        (bucket_table()[:, :, None] == np.arange(BUCKETS)[None, None, :]).astype(np.float32)
    )
    visible = jnp.arange(LEN)[None, :] < lengths[:, None]
    hidden = hidden_states
    gathered = lax.all_gather(hidden, "mp", axis=1, tiled=True)
    normed = normed_rows(gathered, norm_gain[0])
    zero_queries = jnp.zeros((tokens_here, inner_here), jnp.float32)
    zero_pairs = jnp.zeros((2, tokens_here, inner_here), jnp.float32)
    query_rows = query_weight[0]
    pair_rows = keyvalue_weight[0]
    out_rows = output_weight[0]
    shard_rows = side_by_side((query_rows, pair_rows, out_rows), "dp", 0, 1)
    query_acc, pair_acc = add_projections(
        zero_queries, zero_pairs, normed, shard_rows[0], shard_rows[1]
    )
    whole_rows = shard_rows[2]
    query_acc, pair_acc, out_full = (query_acc, pair_acc, whole_rows)
    queries = query_acc.astype(jnp.bfloat16).reshape(captions, LEN, heads_here, DH)
    key_rows = pair_acc[0].astype(jnp.bfloat16).reshape(captions, LEN, heads_here, DH)
    value_rows = pair_acc[1].astype(jnp.bfloat16).reshape(captions, LEN, heads_here, DH)
    position_terms = jnp.einsum(
        "qkb,bh->hqk", bucket_onehot, position_bias[0], precision=lax.Precision.HIGHEST
    )
    scores = (
        jnp.einsum("cqhe,ckhe->chqk", queries, key_rows, preferred_element_type=jnp.float32)
        + position_terms[None]
    )
    scores = jnp.where(visible[:, None, None, :], scores, -1e30)
    maxima = jnp.max(scores, axis=-1, keepdims=True)
    raised = jnp.exp(scores - maxima)
    weights = (raised / jnp.sum(raised, axis=-1, keepdims=True)).astype(jnp.bfloat16)
    mixture = jnp.einsum("chqk,ckhe->cqhe", weights, value_rows, preferred_element_type=jnp.float32)
    attended = mixture.astype(jnp.bfloat16).reshape(tokens_here, inner_here)
    partial_out = jnp.einsum("tf,df->td", attended, out_full, preferred_element_type=jnp.float32)
    reduced = lax.psum_scatter(
        partial_out.astype(jnp.bfloat16), "mp", scatter_dimension=1, tiled=True
    ).astype(jnp.float32)
    hidden = (hidden.astype(jnp.float32) + reduced).astype(jnp.bfloat16)
    return hidden


def solution(mesh):
    in_specs = (
        P("dp", "mp"),
        P(),
        P(None, "dp", "mp"),
        P(None, "dp", None, "mp"),
        P(None, "dp", "mp"),
        P(None, None, "mp"),
        P("dp"),
    )
    out_specs = P("dp", "mp")
    return jax.shard_map(local, mesh=mesh, in_specs=in_specs, out_specs=out_specs, check_vma=False)
```

profile of v0, /device:TPU:65, one launch (start us, length us, event | category | flops | bytes accessed | tf_op | source)
XLA Modules:
  0.0 413.0 jit_solution(2870992319001672972)
XLA Ops:
  6.5 0.0 copy-start
  6.5 0.0 copy-start.2
  6.5 0.0 copy-start.5
  6.5 0.0 all-gather.5.cloned.1.call-start
  6.5 0.7 all-gather.5.cloned.1.call-update
  7.3 0.0 all-gather.3.cloned.1.call-start
  7.3 1.2 copy.28
  8.5 1.0 copy.17
  9.5 1.0 copy.19
  10.5 0.8 pad_maximum_fusion
  11.4 0.0 all-gather.3.cloned.1.call-update
  11.4 0.0 reduce-scatter.2.cloned.1.call-start
  11.4 0.0 copy-done
  11.4 0.0 copy-done.2
  11.4 1.2 convolution_bitcast_fusion
  12.7 0.2 copy.23
  12.9 0.0 copy-done.5
  12.9 0.1 iota_compare_fusion
  13.0 51.6 %all-gather.5.cloned.1.call-done = bf16[512,4096]{1,0:T(8,128)(2,1)} async-done(((bf16[512,512]{1,0:T(8,128)(2,1)}), bf16[512,4096]{1,0:T(8,128)(2,1)}) %all-gather.5.cloned.1.call-update) | async-done | bytes 4194320 | tf_op jit(solution)/shard_map/all_gather | solution.py:65
  64.6 3.1 fusion.1
  67.6 0.0 copy-start.4
  67.7 222.8 %all-gather.3.cloned.1.call-done = bf16[4096,2048]{0,1:T(8,128)(2,1)} async-done(((bf16[128,2048]{0,1:T(8,128)(2,1)}), bf16[4096,2048]{0,1:T(8,128)(2,1)}) %all-gather.3.cloned.1.call-update) | async-done | bytes 16777232 | tf_op jit(solution)/shard_map/all_gather | solution.py:17
  290.5 0.0 copy-start.1
  290.5 7.9 %slice.22 = bf16[4096,1024]{0,1:T(8,128)(2,1)} slice(bf16[4096,2048]{0,1:T(8,128)(2,1)} %all-gather.3.cloned.1.call-done), slice={[0:4096], [512:1536]} | slice | bytes 16777216 | tf_op jit(solution)/shard_map/slice | solution.py:19
  298.4 0.0 copy-done.4
  298.4 0.0 copy-done.1
  298.4 7.3 %fusion.13 = bf16[2,512,512]{1,2,0:T(8,128)(2,1)S(1)} fusion(bf16[4096,2,512]{0,2,1:T(8,128)(2,1)} %bitcast.35, bf16[512,4096]{1,0:T(8,128)(2,1)S(1)} %copy-done.1, f32[4096]{0:T(1024)S(1)} %bitcast.40, f32[512]{0:T(512)S(1)} %add_rsqrt_fusion), kind=kOutput, calls=%fused_computation.17 | convolution fusion | flops 4303880192 | bytes 13649920 | tf_op jit(solution)/shard_map/td,dcf->ctf/dot_general | solution.py:49
  305.7 0.1 fusion.45
  305.8 0.1 convert_element_type.45
  305.9 5.8 %fusion.16 = bf16[512,512]{1,0:T(8,128)(2,1)S(1)} fusion(bf16[4096,2048]{0,1:T(8,128)(2,1)} %all-gather.3.cloned.1.call-done, bf16[512,4096]{1,0:T(8,128)(2,1)} %all-gather.5.cloned.1.call-done, f32[4096]{0:T(1024)S(1)} %bitcast.41, f32[512]{0:T(512)S(1)} %add_rsqrt_fusion), kind=kOutput, calls=%fused_computation.18 | convolution fusion | flops 2156134400 | bytes 8931328 | tf_op jit(solution)/shard_map/dot_general | solution.py:48
  311.7 0.5 reshape.48
  312.3 0.1 convert_element_type.43
  312.4 2.5 fusion.46
  315.0 2.0 fusion.19
  317.0 0.4 copy.26
  317.4 6.5 %convolution_convert_fusion = bf16[512,4096]{1,0:T(8,128)(2,1)} fusion(bf16[4096,2048]{0,1:T(8,128)(2,1)} %all-gather.3.cloned.1.call-done, bf16[64,8,4,128]{3,2,1,0:T(4,128)(2,1)S(1)} %bitcast.36), kind=kOutput, calls=%fused_computation.6 | convolution fusion | flops 2149580800 | bytes 8912896 | tf_op jit(solution)/shard_map/tf,df->td/dot_general | solution.py:94
  323.9 0.0 copy-start.3
  323.9 0.0 reduce-scatter.2.cloned.1.call-update
  323.9 80.5 %reduce-scatter.2.cloned.1.call-done = bf16[512,512]{1,0:T(8,128)(2,1)} async-done(((bf16[512,4096]{1,0:T(8,128)(2,1)}), bf16[512,512]{1,0:T(8,128)(2,1)}) %reduce-scatter.2.cloned.1.call-update) | async-done | bytes 524304 | tf_op jit(solution)/shard_map/reduce_scatter | solution.py:95
  404.4 0.0 copy-done.3
  404.4 2.0 add_convert_fusion
  (1 shorter events, 0.0 us)
Async XLA Ops:
  6.5 4.9 %copy-start = (f32[1,32,8]{1,2,0:T(8,128)S(1)}, f32[1,32,8]{1,2,0:T(8,128)}, u32[]{:S(2)}) copy-start(f32[1,32,8]{1,2,0:T(8,128)} %param.13) | copy-start | bytes 3076
  6.5 4.9 %copy-start.2 = (f32[128,128,32]{1,2,0:T(8,128)S(1)}, f32[128,128,32]{1,2,0:T(8,128)}, u32[]{:S(2)}) copy-start(f32[128,128,32]{1,2,0:T(8,128)} %constant.13.clone) | copy-start | bytes 6291460
  6.5 6.4 %copy-start.5 = (s32[4]{0:T(128)S(1)}, s32[4]{0:T(128)}, u32[]{:S(2)}) copy-start(s32[4]{0:T(128)} %param.14) | copy-start | bytes 52
  6.5 58.0 %all-gather.5.cloned.1.call-start = ((), (), s32[]{:S(2)}) async-start(), calls=%async_computation.2 | async-start | bytes 4718592 | tf_op jit(solution)/shard_map/all_gather | solution.py:65
  7.3 283.2 %all-gather.3.cloned.1.call-start = ((), (), s32[]{:S(2)}) async-start(), calls=%async_computation.1 | async-start | bytes 17301504 | tf_op jit(solution)/shard_map/all_gather | solution.py:17
  11.4 393.1 %reduce-scatter.2.cloned.1.call-start = ((), (), s32[]{:S(2)}) async-start(), calls=%async_computation.3 | async-start | bytes 4718592 | tf_op jit(solution)/shard_map/reduce_scatter | solution.py:95
  67.6 230.7 %copy-start.4 = (f32[1,4096]{1,0:T(1,128)S(1)}, f32[1,4096]{1,0:T(1,128)}, u32[]{:S(2)}) copy-start(f32[1,4096]{1,0:T(1,128)} %param.9) | copy-start | bytes 49156
  290.5 7.9 %copy-start.1 = (bf16[512,4096]{1,0:T(8,128)(2,1)S(1)}, bf16[512,4096]{1,0:T(8,128)(2,1)}, u32[]{:S(2)}) copy-start(bf16[512,4096]{1,0:T(8,128)(2,1)} %all-gather.5.cloned.1.call-done) | copy-start | bytes 12582916
  323.9 80.5 %copy-start.3 = (bf16[512,512]{1,0:T(8,128)(2,1)S(1)}, bf16[512,512]{1,0:T(8,128)(2,1)}, u32[]{:S(2)}) copy-start(bf16[512,512]{1,0:T(8,128)(2,1)} %param.8) | copy-start | bytes 1572868
Sparse Core Ops, SparseCore 0:
  9.2 55.3 all-gather.4
  66.3 224.1 all-gather.2
  324.1 80.3 reduce-scatter.1
where the time goes:
time: 413 us
  waiting for transfers between devices  356 us (86%)
  matrix products  25.4 us (6%)
  between operations  13.2 us (3%)
  local copies, waits for them, and re-layouts  12.6 us (3%)
  other arithmetic  6 us (1%)
    all_gather x1, waiting for transfers between devices, side_by_side(): filled, at, outs = (lax.all_gather(both, axis, axis=dim, tiled=True), 0, [])  223 us
    reduce_scatter x1, waiting for transfers between devices, local(): lax.psum_scatter(partial_out.astype(jnp.bfloat16), 'mp', scatter_dimensio...  80.5 us
    all_gather x1, waiting for transfers between devices, local(): gathered = lax.all_gather(hidden, 'mp', axis=1, tiled=True)  51.6 us
  transfers between devices with their start and end apart: 3, of which 3 were waited for; matrix products, arithmetic and copies ran while one was open for 2% of the time, Pallas kernels for 0%

commit v1 on v0

--- a/solution.py
+++ b/solution.py
@@ -62,7 +62,9 @@
     )
     visible = jnp.arange(LEN)[None, :] < lengths[:, None]
     hidden = hidden_states
-    gathered = lax.all_gather(hidden, "mp", axis=1, tiled=True)
+    gathered = jnp.concatenate(
+        lax.all_to_all(jnp.stack([hidden] * lax.axis_size("mp")), "mp", 0, 0), axis=1
+    )
     normed = normed_rows(gathered, norm_gain[0])
     zero_queries = jnp.zeros((tokens_here, inner_here), jnp.float32)
     zero_pairs = jnp.zeros((2, tokens_here, inner_here), jnp.float32)

time: 413 us -> 436 us (1.056)
  local copies, waits for them, and re-layouts: 12.6 us -> 23.1 us
  starting transfers between devices: 0.08 us -> 8.53 us
  other arithmetic: 6 us -> 11.8 us
    all_to_all x0 -> x1, waiting for transfers between devices: none -> 128 us  [local(): lax.all_to_all(jnp.stack([hidden] * lax.axis_size('mp')), 'mp', 0, 0)]
    all_gather x1, waiting for transfers between devices: 223 us -> 149 us  [side_by_side(): filled, at, outs = (lax.all_gather(both, axis, axis=dim, tiled=True), 0, [])]
    all_gather x1 -> x0, waiting for transfers between devices: 51.6 us -> none  [local(): gathered = lax.all_gather(hidden, 'mp', axis=1, tiled=True)]
    all_to_all x0 -> x1, starting transfers between devices: none -> 8.53 us  [local(): lax.all_to_all(jnp.stack([hidden] * lax.axis_size('mp')), 'mp', 0, 0)]
    all_to_all x0 -> x1, local copies, waits for them, and re-layouts: none -> 6.5 us  [local(): lax.all_to_all(jnp.stack([hidden] * lax.axis_size('mp')), 'mp', 0, 0)]
    reduce_scatter x1, waiting for transfers between devices: 80.5 us -> 75.3 us  [local(): lax.psum_scatter(partial_out.astype(jnp.bfloat16), 'mp', scatter_dimensio...]
  transfers between devices with their start and end apart: 3 -> 3, of which waited for: 3 -> 3; matrix products, arithmetic and copies ran while one was open for 2% -> 5% of each run, Pallas kernels for 0% -> 0%
where the time goes in v1:
time: 436 us; the launch traced here: 435 us
  waiting for transfers between devices  353 us (81%)
  matrix products  25.4 us (6%)
  local copies, waits for them, and re-layouts  23.1 us (5%)
  between operations  13.5 us (3%)
  other arithmetic  11.8 us (3%)
  starting transfers between devices  8.53 us (2%)
    all_gather x1, waiting for transfers between devices, side_by_side(): filled, at, outs = (lax.all_gather(both, axis, axis=dim, tiled=True), 0, [])  149 us
    all_to_all x1, waiting for transfers between devices, local(): lax.all_to_all(jnp.stack([hidden] * lax.axis_size('mp')), 'mp', 0, 0)  128 us
    reduce_scatter x1, waiting for transfers between devices, local(): lax.psum_scatter(partial_out.astype(jnp.bfloat16), 'mp', scatter_dimensio...  75.3 us
  transfers between devices with their start and end apart: 3, of which 3 were waited for; matrix products, arithmetic and copies ran while one was open for 5% of the time, Pallas kernels for 0%

profile of v1, /device:TPU:65, one launch (start us, length us, event | category | flops | bytes accessed | tf_op | source)
XLA Modules:
  0.0 435.0 jit_solution(18194182420709615815)
XLA Ops:
  6.5 0.0 copy-start
  6.5 0.0 all-gather.2.cloned.1.call-start
  6.5 1.0 copy.37
  7.6 1.0 copy.39
  8.6 1.2 copy.51
  9.8 0.8 pad_maximum_fusion
  10.6 0.0 all-gather.2.cloned.1.call-update
  10.6 3.4 stack.2
  14.0 0.0 copy-start.5
  14.0 0.0 copy-start.4
  14.0 0.0 copy-start.6
  14.0 8.5 %all-to-all-start = ((bf16[8,512,512]{2,1,0:T(8,128)(2,1)}), bf16[8,512,512]{2,1,0:T(8,128)(2,1)}, u32[]{:S(2)}, u32[]{:S(2)}) async-start(bf16[8,512,512]{2,1,0:T(8,128)(2,1)} %stack.2), calls=%async_computation | async-start | bytes 8388608 | tf_op jit(solution)/shard_map/all_to_all | solution.py:66
  22.5 0.0 reduce-scatter.2.cloned.1.call-start
  22.5 0.5 broadcast.36
  23.0 0.0 copy-done.5
  23.1 0.6 reduce.5
  23.7 0.0 copy-done
  23.7 0.0 copy-done.4
  23.7 1.2 convolution_bitcast_fusion
  24.9 0.2 copy.45
  25.2 0.0 copy-done.6
  25.2 0.1 iota_compare_fusion
  25.2 127.9 %all-to-all-done = bf16[8,512,512]{2,1,0:T(8,128)(2,1)} async-done(((bf16[8,512,512]{2,1,0:T(8,128)(2,1)}), bf16[8,512,512]{2,1,0:T(8,128)(2,1)}, u32[]{:S(2)}, u32[]{:S(2)}) %all-to-all-start) | async-done | bytes 4194336 | tf_op jit(solution)/shard_map/all_to_all | solution.py:66
  153.1 6.5 %copy.40 = bf16[8,512,512]{1,2,0:T(8,128)(2,1)} copy(bf16[8,512,512]{2,1,0:T(8,128)(2,1)} %all-to-all-done) | data formatting | bytes 8388608 | tf_op jit(solution)/shard_map/all_to_all | solution.py:66
  159.6 0.0 copy-start.1
  159.6 3.3 multiply_reduce_fusion
  162.9 0.2 copy-done.1
  163.1 2.6 multiply_convert_fusion
  165.6 2.5 fusion.2
  168.1 149.4 %all-gather.2.cloned.1.call-done = bf16[4096,2048]{0,1:T(8,128)(2,1)} async-done(((bf16[128,2048]{0,1:T(8,128)(2,1)}), bf16[4096,2048]{0,1:T(8,128)(2,1)}) %all-gather.2.cloned.1.call-update) | async-done | bytes 16777232 | tf_op jit(solution)/shard_map/all_gather | solution.py:17
  317.5 5.8 %fusion.8 = bf16[512,512]{1,0:T(8,128)(2,1)S(1)} fusion(bf16[512,4096]{0,1:T(8,128)(2,1)} %fusion.2, bf16[4096,2048]{0,1:T(8,128)(2,1)} %all-gather.2.cloned.1.call-done), kind=kOutput, calls=%fused_computation.16 | convolution fusion | flops 2147745792 | bytes 8912896 | tf_op jit(solution)/shard_map/dot_general | solution.py:48
  323.4 0.5 reshape.66
  323.9 0.0 copy-start.2
  323.9 7.9 %slice.22 = bf16[4096,1024]{0,1:T(8,128)(2,1)} slice(bf16[4096,2048]{0,1:T(8,128)(2,1)} %all-gather.2.cloned.1.call-done), slice={[0:4096], [512:1536]} | slice | bytes 16777216 | tf_op jit(solution)/shard_map/slice | solution.py:19
  331.8 0.0 copy-done.2
  331.8 7.3 %fusion.7 = bf16[2,512,512]{1,2,0:T(8,128)(2,1)S(1)} fusion(bf16[4096,2,512]{0,2,1:T(8,128)(2,1)} %bitcast.43, bf16[512,4096,1]{0,1,2:T(8,128)(2,1)S(1)} %bitcast.44), kind=kOutput, calls=%fused_computation.15 | convolution fusion | flops 4295491584 | bytes 13631488 | tf_op jit(solution)/shard_map/td,dcf->ctf/dot_general | solution.py:49
  339.1 0.1 fusion.35
  339.1 0.1 convert_element_type.57
  339.3 0.1 convert_element_type.63
  339.4 2.5 fusion.36
  341.9 2.0 fusion.11
  344.0 0.4 copy.48
  344.4 6.5 %convolution_convert_fusion = bf16[512,4096]{1,0:T(8,128)(2,1)} fusion(bf16[4096,2048]{0,1:T(8,128)(2,1)} %all-gather.2.cloned.1.call-done, bf16[64,8,4,128]{3,2,1,0:T(4,128)(2,1)S(1)} %bitcast.45), kind=kOutput, calls=%fused_computation.6 | convolution fusion | flops 2149580800 | bytes 8912896 | tf_op jit(solution)/shard_map/tf,df->td/dot_general | solution.py:96
  350.9 0.0 copy-start.3
  350.9 0.0 reduce-scatter.2.cloned.1.call-update
  350.9 75.3 %reduce-scatter.2.cloned.1.call-done = bf16[512,512]{1,0:T(8,128)(2,1)} async-done(((bf16[512,4096]{1,0:T(8,128)(2,1)}), bf16[512,512]{1,0:T(8,128)(2,1)}) %reduce-scatter.2.cloned.1.call-update) | async-done | bytes 524304 | tf_op jit(solution)/shard_map/reduce_scatter | solution.py:97
  426.2 0.0 copy-done.3
  426.2 2.0 add_convert_fusion
  (2 shorter events, 0.0 us)
Async XLA Ops:
  6.5 17.1 %copy-start = (f32[1,32,8]{1,2,0:T(8,128)S(1)}, f32[1,32,8]{1,2,0:T(8,128)}, u32[]{:S(2)}) copy-start(f32[1,32,8]{1,2,0:T(8,128)} %param.13) | copy-start | bytes 3076
  6.5 311.0 %all-gather.2.cloned.1.call-start = ((), (), s32[]{:S(2)}) async-start(), calls=%async_computation.2 | async-start | bytes 17301504 | tf_op jit(solution)/shard_map/all_gather | solution.py:17
  14.0 9.1 %copy-start.5 = (f32[1,4096]{1,0:T(1,128)S(1)}, f32[1,4096]{1,0:T(1,128)}, u32[]{:S(2)}) copy-start(f32[1,4096]{1,0:T(1,128)} %param.9) | copy-start | bytes 49156
  14.0 9.7 %copy-start.4 = (f32[128,128,32]{1,2,0:T(8,128)S(1)}, f32[128,128,32]{1,2,0:T(8,128)}, u32[]{:S(2)}) copy-start(f32[128,128,32]{1,2,0:T(8,128)} %constant.13.clone) | copy-start | bytes 6291460
  14.0 11.2 %copy-start.6 = (s32[4]{0:T(128)S(1)}, s32[4]{0:T(128)}, u32[]{:S(2)}) copy-start(s32[4]{0:T(128)} %param.14) | copy-start | bytes 52
  14.0 139.1 %all-to-all-start = ((bf16[8,512,512]{2,1,0:T(8,128)(2,1)}), bf16[8,512,512]{2,1,0:T(8,128)(2,1)}, u32[]{:S(2)}, u32[]{:S(2)}) async-start(bf16[8,512,512]{2,1,0:T(8,128)(2,1)} %stack.2), calls=%async_computation | async-start | bytes 8388608 | tf_op jit(solution)/shard_map/all_to_all | solution.py:66
  22.5 403.7 %reduce-scatter.2.cloned.1.call-start = ((), (), s32[]{:S(2)}) async-start(), calls=%async_computation.3 | async-start | bytes 4718592 | tf_op jit(solution)/shard_map/reduce_scatter | solution.py:97
  159.6 3.4 copy-start.1
  323.9 7.9 %copy-start.2 = (bf16[8,512,512]{1,2,0:T(8,128)(2,1)S(1)}, bf16[8,512,512]{1,2,0:T(8,128)(2,1)}, u32[]{:S(2)}) copy-start(bf16[8,512,512]{1,2,0:T(8,128)(2,1)} %multiply_convert_fusion) | copy-start | bytes 12582916
  350.9 75.3 %copy-start.3 = (bf16[512,512]{1,0:T(8,128)(2,1)S(1)}, bf16[512,512]{1,0:T(8,128)(2,1)}, u32[]{:S(2)}) copy-start(bf16[512,512]{1,0:T(8,128)(2,1)} %param.8) | copy-start | bytes 1572868
Sparse Core Ops, SparseCore 0:
  10.7 306.7 all-gather.1
  351.0 75.1 reduce-scatter.1
